TPU v7x, 256 devices: a whole 4x4x8 slice. The times are simulated.
256 devices in a mesh: dp: 2 (over z_hi), group: 16 (over x, y), seq: 8 (over z_lo, core).
Axes of the slice: x: 4, y: 4, z: 8 (z_hi: 2, z_lo: 4; z = z_hi * 4 + z_lo), core: 2. Of those that a mesh axis runs over, the one named last changes fastest.
Arguments:
- queries: bfloat16 [2, 4096, 2560], P('dp', 'group', 'seq'), may hold values from -6 to 6
- keys: bfloat16 [2, 4096, 2560], P('dp', 'group', 'seq'), may hold values from -6 to 6
- values: bfloat16 [2, 4096, 2560], P('dp', 'group', 'seq'), may hold values from -6 to 6
- cotangent: bfloat16 [2, 4096, 2560], P('dp', 'group', 'seq'), may hold values from -18 to 18
- level_bias: float32 [3, 40], P(None, 'seq'), may hold values from -3 to 3
- off_mid: int32 [40], P('seq'), may hold values from 0 to 7
- off_far: int32 [40], P('seq'), may hold values from 0 to 63
Outputs:
- attended: bfloat16 [2, 4096, 2560], P('dp', 'group', 'seq')
- query_grad: bfloat16 [2, 4096, 2560], P('dp', 'group', 'seq')
- key_grad: bfloat16 [2, 4096, 2560], P('dp', 'group', 'seq')
- value_grad: bfloat16 [2, 4096, 2560], P('dp', 'group', 'seq')
- bias_grad: float32 [3, 40], replicated
All inputs are finite; a program needn't handle non-finite values.
Results may differ from a plain program's by a relative error of at most 0.04.
Values may be sent and summed in bfloat16 or wider, within the bound.
No kernel may reach another device: no remote copies, remote signals or barrier semaphores. Data moves between devices by JAX's collectives and lax.ppermute only.
A program may use at most 64 MiB of HBM per device.

v0:
```python
import math
import jax
import jax.numpy as jnp
from jax import lax
from jax.sharding import Mesh
from jax.sharding import PartitionSpec as P

HEADS = 40
R_MID = 8
R_FAR = 64
GROUP = ("group_0", "group_1")
SEQ = ("seq_0", "seq_1")
DP_GROUP_SEQ = ("dp", "group_0", "group_1", "seq_0", "seq_1")


def sent_together(arrays, axis, dim, along):
    widths = [a.shape[along] for a in arrays]
    both = jnp.concatenate(arrays, axis=along)
    filled = lax.all_gather(both, axis, axis=dim, tiled=True)
    return tuple(jnp.split(filled, [sum(widths[:k]) for k in range(1, len(widths))], axis=along))


def one_axis_at_a_time(array, axes):
    for axis in axes:
        array = lax.psum(array, axis)
    return array


def split_up(array, dim, count):
    before, after = (array.shape[:dim], array.shape[dim + 1 :])
    return jnp.moveaxis(array.reshape(*before, count, -1, *after), dim, 0)


def sent_and_summed(array, axis, dim):
    count = lax.axis_size(axis)
    pieces = lax.all_to_all(split_up(array, dim, count), axis, 0, 0, tiled=True)
    return jnp.sum(pieces.astype(jnp.float32), axis=0)


def side_by_side(arrays, axis, dim, along):
    ends, at = ([], 0)
    for a in arrays[:-1]:
        at += a.shape[along]
        ends.append(at)
    both = jnp.concatenate(arrays, axis=along)
    return tuple(jnp.split(sent_and_summed(both, axis, dim), ends, axis=along))


def select_rows(source, stride, offsets):
    count = source.shape[0] // stride
    shaped = source.reshape((count, stride) + source.shape[1:])
    picker = offsets.reshape((1, 1, -1) + (1,) * (source.ndim - 2))
    picker = jnp.broadcast_to(picker, (count, 1) + source.shape[1:])
    return jnp.take_along_axis(shaped, picker, axis=1)[:, 0]


def place_rows(source, stride, offsets, filler):
    heads = source.shape[1]
    marked = jnp.arange(stride, dtype=jnp.int32)[:, None] == offsets[None, :]
    marked = marked.reshape((1, stride, heads) + (1,) * (source.ndim - 2))
    spread = jnp.where(marked, source[:, None], jnp.asarray(filler, source.dtype))
    return spread.reshape((source.shape[0] * stride,) + source.shape[1:])


def forward_level(queries, keys, values, visible, scaling):
    scores = jnp.einsum("qhe,khe->hqk", queries, keys, preferred_element_type=jnp.float32) * scaling
    scores = jnp.where(visible[None], scores, -jnp.inf)
    highest = jnp.max(scores, axis=2, keepdims=True)
    log_sum = highest + jnp.log(jnp.sum(jnp.exp(scores - highest), axis=2, keepdims=True))
    weights = jnp.exp(scores - log_sum).astype(jnp.bfloat16)
    outputs = jnp.einsum("hqk,khe->qhe", weights, values, preferred_element_type=jnp.float32)
    return (log_sum[:, :, 0].T, outputs)


def backward_level(
    queries, keys, values, cotangent, visible, log_total, row_delta, bias_row, scaling
):
    scores = jnp.einsum("qhe,khe->hqk", queries, keys, preferred_element_type=jnp.float32) * scaling
    shifted = scores + bias_row[:, None, None] - log_total.T[:, :, None]
    weight = jnp.where(visible[None], jnp.exp(jnp.where(visible[None], shifted, 0.0)), 0.0)
    inner = jnp.einsum("qhe,khe->hqk", cotangent, values, preferred_element_type=jnp.float32)
    dscore = weight * (inner - row_delta.T[:, :, None])
    dscore_low = dscore.astype(jnp.bfloat16)
    weight_low = weight.astype(jnp.bfloat16)
    query_part = jnp.einsum("hqk,khe->qhe", dscore_low, keys, preferred_element_type=jnp.float32)
    key_part = jnp.einsum("hqk,qhe->khe", dscore_low, queries, preferred_element_type=jnp.float32)
    value_part = jnp.einsum(
        "hqk,qhe->khe", weight_low, cotangent, preferred_element_type=jnp.float32
    )
    return (query_part, key_part, value_part)


def causal_forward(queries, keys, values, scaling):
    length = queries.shape[0]
    block_rows = min(128, length)
    lse_parts = []
    out_parts = []
    for first_row in range(0, length, block_rows):
        last_row = first_row + block_rows
        query_place = jnp.arange(first_row, last_row, dtype=jnp.int32)
        key_place = jnp.arange(last_row, dtype=jnp.int32)
        visible = key_place[None, :] <= query_place[:, None]
        block_lse, block_out = forward_level(
            queries[first_row:last_row], keys[:last_row], values[:last_row], visible, scaling
        )
        lse_parts.append(block_lse)
        out_parts.append(block_out)
    return (jnp.concatenate(lse_parts, 0), jnp.concatenate(out_parts, 0))


def causal_backward(queries, keys, values, cotangent, log_total, row_delta, bias_row, scaling):
    length = queries.shape[0]
    block_rows = min(128, length)
    query_parts = []
    key_total = jnp.zeros(keys.shape, jnp.float32)
    value_total = jnp.zeros(values.shape, jnp.float32)
    for first_row in range(0, length, block_rows):
        last_row = first_row + block_rows
        query_place = jnp.arange(first_row, last_row, dtype=jnp.int32)
        key_place = jnp.arange(last_row, dtype=jnp.int32)
        visible = key_place[None, :] <= query_place[:, None]
        part_q, part_k, part_v = backward_level(
            queries[first_row:last_row],
            keys[:last_row],
            values[:last_row],
            cotangent[first_row:last_row],
            visible,
            log_total[first_row:last_row],
            row_delta[first_row:last_row],
            bias_row,
            scaling,
        )
        query_parts.append(part_q)
        padding = ((0, length - last_row), (0, 0), (0, 0))
        key_total = key_total + jnp.pad(part_k, padding)
        value_total = value_total + jnp.pad(part_v, padding)
    return (jnp.concatenate(query_parts, 0), key_total, value_total)


def blocked_forward(queries, keys, values, query_start, scaling, block_rows):
    key_place = jnp.arange(keys.shape[0], dtype=jnp.int32)
    query_place = query_start + jnp.arange(0, block_rows, dtype=jnp.int32)
    visible = key_place[None, :] <= query_place[:, None]
    block_lse, block_out = forward_level(queries, keys, values, visible, scaling)
    return (block_lse, block_out)


def blocked_backward(
    queries,
    keys,
    values,
    cotangent,
    log_total,
    row_delta,
    query_start,
    bias_row,
    scaling,
    block_rows,
):
    key_place = jnp.arange(keys.shape[0], dtype=jnp.int32)
    query_place = query_start + jnp.arange(0, block_rows, dtype=jnp.int32)
    visible = key_place[None, :] <= query_place[:, None]
    part_q, part_k, part_v = backward_level(
        queries, keys, values, cotangent, visible, log_total, row_delta, bias_row, scaling
    )
    return (part_q, part_k, part_v)


def per_device(queries, keys, values, cotangent, level_bias, off_mid, off_far):
    tok_rows = queries.shape[1]
    width = queries.shape[2]
    local_heads = level_bias.shape[1]
    head_size = width // local_heads
    scaling = head_size ** (-0.5)
    shape_rows = (tok_rows, local_heads, head_size)
    query_rows = queries[0].reshape(shape_rows)
    key_rows = keys[0].reshape(shape_rows)
    value_rows = values[0].reshape(shape_rows)
    grad_rows = cotangent[0].reshape(shape_rows)
    group_place = lax.axis_index(GROUP)
    anchor = jnp.zeros((), jnp.int32)
    near_lse, near_out = causal_forward(query_rows, key_rows, value_rows, scaling)
    mid_count = tok_rows // R_MID
    mid_start = group_place * mid_count
    mid_block = min(64, mid_count)
    mid_queries = select_rows(query_rows, R_MID, off_mid)
    mid_keys = select_rows(key_rows, R_MID, off_mid)
    mid_values = select_rows(value_rows, R_MID, off_mid)
    mid_all_keys, mid_all_values = (
        lax.all_gather(mid_keys, GROUP, axis=0, tiled=True),
        lax.all_gather(mid_values, GROUP, axis=0, tiled=True),
    )
    mid_lse, mid_out = blocked_forward(
        mid_queries, mid_all_keys, mid_all_values, mid_start, scaling, mid_block
    )
    far_count = tok_rows // R_FAR
    far_start = group_place * far_count
    far_queries = select_rows(query_rows, R_FAR, off_far)
    far_keys = select_rows(key_rows, R_FAR, off_far)
    far_values = select_rows(value_rows, R_FAR, off_far)
    far_all_keys, far_all_values = sent_together((far_keys, far_values), GROUP, 0, 1)
    far_lse, far_out = blocked_forward(
        far_queries, far_all_keys, far_all_values, far_start, scaling, far_count
    )
    gate_near = near_lse + level_bias[0][None, :]
    gate_mid = place_rows(mid_lse, R_MID, off_mid, -jnp.inf) + level_bias[1][None, :]
    gate_far = place_rows(far_lse, R_FAR, off_far, -jnp.inf) + level_bias[2][None, :]
    highest = jnp.maximum(gate_near, jnp.maximum(gate_mid, gate_far))
    log_total = highest + jnp.log(
        jnp.exp(gate_near - highest) + jnp.exp(gate_mid - highest) + jnp.exp(gate_far - highest)
    )
    share_near = jnp.exp(gate_near - log_total)
    share_mid = jnp.exp(gate_mid - log_total)
    share_far = jnp.exp(gate_far - log_total)
    mid_full = place_rows(mid_out, R_MID, off_mid, 0.0)
    far_full = place_rows(far_out, R_FAR, off_far, 0.0)
    mixed = (
        share_near[..., None] * near_out
        + share_mid[..., None] * mid_full
        + share_far[..., None] * far_full
    )
    attended = mixed.astype(jnp.bfloat16)
    grad_float = grad_rows.astype(jnp.float32)
    row_delta = jnp.sum(grad_float * attended.astype(jnp.float32), axis=2)
    level_terms = jnp.stack(
        [
            jnp.sum(share_near * (jnp.sum(grad_float * near_out, axis=2) - row_delta), axis=0),
            jnp.sum(share_mid * (jnp.sum(grad_float * mid_full, axis=2) - row_delta), axis=0),
            jnp.sum(share_far * (jnp.sum(grad_float * far_full, axis=2) - row_delta), axis=0),
        ]
    )
    placed_terms = lax.dynamic_update_slice(
        jnp.zeros((3, HEADS), jnp.float32), level_terms, (anchor, lax.axis_index(SEQ) * local_heads)
    )
    bias_total = one_axis_at_a_time(placed_terms, DP_GROUP_SEQ)
    near_dq, near_dk, near_dv = causal_backward(
        query_rows, key_rows, value_rows, grad_rows, log_total, row_delta, level_bias[0], scaling
    )
    mid_grads = select_rows(grad_rows, R_MID, off_mid)
    mid_total = select_rows(log_total, R_MID, off_mid)
    mid_delta = select_rows(row_delta, R_MID, off_mid)
    mid_dq, mid_dk_terms, mid_dv_terms = blocked_backward(
        mid_queries,
        mid_all_keys,
        mid_all_values,
        mid_grads,
        mid_total,
        mid_delta,
        mid_start,
        level_bias[1],
        scaling,
        mid_block,
    )
    mid_dk, mid_dv = side_by_side(
        (mid_dk_terms.astype(jnp.bfloat16), mid_dv_terms.astype(jnp.bfloat16)), GROUP, 0, 1
    )
    far_grads = select_rows(grad_rows, R_FAR, off_far)
    far_total = select_rows(log_total, R_FAR, off_far)
    far_delta = select_rows(row_delta, R_FAR, off_far)
    far_dq, far_dk_terms, far_dv_terms = blocked_backward(
        far_queries,
        far_all_keys,
        far_all_values,
        far_grads,
        far_total,
        far_delta,
        far_start,
        level_bias[2],
        scaling,
        far_count,
    )
    far_dk, far_dv = side_by_side(
        (far_dk_terms.astype(jnp.bfloat16), far_dv_terms.astype(jnp.bfloat16)), GROUP, 0, 1
    )
    query_grad = scaling * (
        near_dq + place_rows(mid_dq, R_MID, off_mid, 0.0) + place_rows(far_dq, R_FAR, off_far, 0.0)
    )
    key_grad = scaling * (
        near_dk + place_rows(mid_dk, R_MID, off_mid, 0.0) + place_rows(far_dk, R_FAR, off_far, 0.0)
    )
    value_grad = (
        near_dv + place_rows(mid_dv, R_MID, off_mid, 0.0) + place_rows(far_dv, R_FAR, off_far, 0.0)
    )
    bias_grad = bias_total / math.sqrt(lax.axis_size("dp") * lax.axis_size(GROUP) * tok_rows)
    out_shape = (1, tok_rows, width)
    return (
        attended.reshape(out_shape),
        query_grad.astype(jnp.bfloat16).reshape(out_shape),
        key_grad.astype(jnp.bfloat16).reshape(out_shape),
        value_grad.astype(jnp.bfloat16).reshape(out_shape),
        bias_grad,
    )


def solution(mesh):
    finer = Mesh(
        mesh.devices.reshape(mesh.shape["dp"], 4, 4, 4, 2),
        ("dp", "group_0", "group_1", "seq_0", "seq_1"),
    )
    in_specs = (
        P("dp", GROUP, SEQ),
        P("dp", GROUP, SEQ),
        P("dp", GROUP, SEQ),
        P("dp", GROUP, SEQ),
        P(None, SEQ),
        P(SEQ),
        P(SEQ),
    )
    out_specs = (
        P("dp", GROUP, SEQ),
        P("dp", GROUP, SEQ),
        P("dp", GROUP, SEQ),
        P("dp", GROUP, SEQ),
        P(),
    )
    return jax.shard_map(
        per_device, mesh=finer, in_specs=in_specs, out_specs=out_specs, check_vma=False
    )
```

profile of v0, /device:TPU:8, one launch (start us, length us, event | category | flops | bytes accessed | tf_op | source)
XLA Modules:
  0.0 704.0 jit_solution(6368570354909001349)
XLA Ops:
  3.4 1.1 reshape_reshape_squeeze.26
  4.5 1.1 copy.273
  5.6 1.2 reshape_reshape_squeeze.27
  10.2 13.7 %gather_fusion.2 = bf16[1280]{0:T(1024)(128)(2,1)S(1)} fusion(bf16[4,64,5,64]{1,0,3,2:T(4,128)(2,1)S(1)} %reshape_reshape_squeeze.26, s32[1280]{0:T(1024)S(1)} %reshape.1163), kind=kCustom, calls=%fused_computation.1.clone | custom fusion | bytes 25600 | tf_op jit(solution)/shard_map/jit(take_along_axis)/gather | solution.py:54
  23.9 13.7 %gather_fusion.3 = bf16[1280]{0:T(1024)(128)(2,1)S(1)} fusion(bf16[4,64,5,64]{1,0,3,2:T(4,128)(2,1)S(1)} %reshape_reshape_squeeze.27, s32[1280]{0:T(1024)S(1)} %reshape.1163), kind=kCustom, calls=%fused_computation.7.clone | custom fusion | bytes 25600 | tf_op jit(solution)/shard_map/jit(take_along_axis)/gather | solution.py:54
  37.7 13.7 %gather_fusion.4 = bf16[1280]{0:T(1024)(128)(2,1)S(1)} fusion(bf16[4,64,5,64]{1,0,3,2:T(4,128)(2,1)S(1)} %reshape_reshape_squeeze.28, s32[1280]{0:T(1024)S(1)} %reshape.1163), kind=kCustom, calls=%fused_computation.8.clone | custom fusion | bytes 25600 | tf_op jit(solution)/shard_map/jit(take_along_axis)/gather | solution.py:54
  51.5 13.7 %gather_fusion.10 = bf16[1280]{0:T(1024)(128)(2,1)S(1)} fusion(bf16[4,64,5,64]{1,0,3,2:T(4,128)(2,1)S(1)} %reshape_reshape_squeeze.31, s32[1280]{0:T(1024)S(1)} %reshape.1163), kind=kCustom, calls=%fused_computation.9.clone | custom fusion | bytes 25600 | tf_op jit(solution)/shard_map/jit(take_along_axis)/gather | solution.py:54
  65.9 23.7 %all_gather.10 = bf16[64,10,64]{2,1,0:T(8,128)(2,1)S(1)} all-gather(bf16[4,10,64]{2,1,0:T(8,128)(2,1)S(1)} %pad_maximum_fusion.3), channel_id=1, replica_groups=mesh['dp'=2,'group_0'=4,'group_1'=4,'seq_0'=4,'seq_1'=2] {'group_0','gro..., dimensions={0}, use_global_device_ids=true | all-gather | bytes 87040 | tf_op jit(solution)/shard_map/all_gather | solution.py:19
  91.6 105.5 %gather_fusion = bf16[10240]{0:T(1024)(128)(2,1)S(1)} fusion(bf16[32,8,5,64]{3,2,1,0:T(8,128)(2,1)S(1)} %reshape_reshape_squeeze.24, s32[10240]{0:T(1024)S(1)} %reshape.1151), kind=kCustom, calls=%fused_computation.clone | custom fusion | bytes 204800 | tf_op jit(solution)/shard_map/jit(take_along_axis)/gather | solution.py:54
  197.4 105.5 %gather_fusion.1 = bf16[10240]{0:T(1024)(128)(2,1)S(1)} fusion(bf16[32,8,5,64]{3,2,1,0:T(8,128)(2,1)S(1)} %reshape_reshape_squeeze.25, s32[10240]{0:T(1024)S(1)} %reshape.1151), kind=kCustom, calls=%fused_computation.4.clone | custom fusion | bytes 204800 | tf_op jit(solution)/shard_map/jit(take_along_axis)/gather | solution.py:54
  303.3 105.5 %gather_fusion.5 = bf16[10240]{0:T(1024)(128)(2,1)S(1)} fusion(bf16[32,8,5,64]{3,2,1,0:T(8,128)(2,1)S(1)} %reshape_reshape_squeeze.29, s32[10240]{0:T(1024)S(1)} %reshape.1151), kind=kCustom, calls=%fused_computation.5.clone | custom fusion | bytes 204800 | tf_op jit(solution)/shard_map/jit(take_along_axis)/gather | solution.py:54
  409.1 105.5 %gather_fusion.7 = bf16[10240]{0:T(1024)(128)(2,1)S(1)} fusion(bf16[32,8,5,64]{3,2,1,0:T(8,128)(2,1)S(1)} %reshape_reshape_squeeze.30, s32[10240]{0:T(1024)S(1)} %reshape.1151), kind=kCustom, calls=%fused_computation.6.clone | custom fusion | bytes 204800 | tf_op jit(solution)/shard_map/jit(take_along_axis)/gather | solution.py:54
  515.5 22.6 %all-gather = bf16[512,1,5,64]{3,0,2,1:T(8,128)(2,1)S(1)} all-gather(bf16[32,1,5,64]{3,0,2,1:T(8,128)(2,1)S(1)} %copy.275), channel_id=2, replica_groups=mesh['dp'=2,'group_0'=4,'group_1'=4,'seq_0'=4,'seq_1'=2] {'group_0','gro..., dimensions={0}, use_global_device_ids=true | all-gather | bytes 348160 | tf_op jit(solution)/shard_map/all_gather | solution.py:190
  542.7 1.1 broadcast_in_dim.438
  543.8 23.1 %all-gather.1 = bf16[512,1,5,64]{3,0,2,1:T(8,128)(2,1)S(1)} all-gather(bf16[32,1,5,64]{3,0,2,1:T(8,128)(2,1)S(1)} %copy.286), channel_id=3, replica_groups=mesh['dp'=2,'group_0'=4,'group_1'=4,'seq_0'=4,'seq_1'=2] {'group_0','gro..., dimensions={0}, use_global_device_ids=true | all-gather | bytes 348160 | tf_op jit(solution)/shard_map/all_gather | solution.py:191
  567.0 0.9 convolution_bitcast_fusion.5
  568.6 0.9 broadcast_bitcast_fusion.2
  569.5 2.0 copy.296
  571.5 1.9 fusion.37
  573.4 1.8 fusion.49
  575.6 1.5 fusion.35
  577.1 1.6 multiply_reduce_fusion.2
  579.7 0.8 copy.302
  581.8 0.9 gather_fusion.9
  582.9 0.9 gather_fusion.11
  584.7 0.9 fusion.18
  585.6 1.1 fusion.20
  588.0 1.7 copy.328
  589.7 1.6 copy.392
  591.3 1.7 reshape.1221
  593.0 5.6 all-to-all-start.1
  601.0 2.2 gather_fusion.6
  603.4 2.7 gather_fusion.8
  607.6 1.2 fusion.8
  608.8 1.3 fusion.16
  610.1 1.2 fusion.7
  611.3 0.9 convolution_bitcast_fusion.4
  612.6 0.9 convolution_bitcast_fusion.3
  613.5 0.8 fusion.121
  614.4 1.1 broadcast_in_dim.434
  617.4 1.7 reshape.1223
  623.8 0.9 copy.290
  624.8 0.9 copy.294
  625.7 1.0 broadcast_in_dim.428.clone
  626.7 1.0 broadcast_in_dim.429
  627.7 1.8 copy.283
  630.3 1.3 broadcast_in_dim.431
  631.7 1.1 copy.293
  632.8 1.3 broadcast_in_dim.426
  634.1 1.7 copy.289
  635.8 2.3 fusion.31
  638.4 10.2 %psum.35 = f32[3,40]{1,0:T(4,128)S(1)} all-reduce(f32[3,40]{1,0:T(4,128)S(1)} %dynamic_update_slice.3), channel_id=1, replica_groups=mesh['dp'=2,'group_0'=4,'group_1'=4,'seq_0'=4,'seq_1'=2] {'dp'}, use_global_device_ids=true, to_apply=%region_17.22 | all-reduce | flops 120 | bytes 960 | tf_op jit(solution)/shard_map/psum | solution.py:25
  648.6 10.4 %psum.36 = f32[3,40]{1,0:T(4,128)S(1)} all-reduce(f32[3,40]{1,0:T(4,128)S(1)} %psum.35), channel_id=1, replica_groups=mesh['dp'=2,'group_0'=4,'group_1'=4,'seq_0'=4,'seq_1'=2] {'group_0'}, use_global_device_ids=true, to_apply=%region_18.23 | all-reduce | flops 120 | bytes 960 | tf_op jit(solution)/shard_map/psum | solution.py:25
  659.0 8.6 %psum.37 = f32[3,40]{1,0:T(4,128)S(1)} all-reduce(f32[3,40]{1,0:T(4,128)S(1)} %psum.36), channel_id=1, replica_groups=mesh['dp'=2,'group_0'=4,'group_1'=4,'seq_0'=4,'seq_1'=2] {'group_1'}, use_global_device_ids=true, to_apply=%region_19.24 | all-reduce | flops 120 | bytes 960 | tf_op jit(solution)/shard_map/psum | solution.py:25
  667.5 11.7 %psum.38 = f32[3,40]{1,0:T(4,128)S(1)} all-reduce(f32[3,40]{1,0:T(4,128)S(1)} %psum.37), channel_id=1, replica_groups=mesh['dp'=2,'group_0'=4,'group_1'=4,'seq_0'=4,'seq_1'=2] {'seq_0'}, use_global_device_ids=true, to_apply=%region_20.25 | all-reduce | flops 120 | bytes 960 | tf_op jit(solution)/shard_map/psum | solution.py:25
  679.2 2.5 psum.39
  681.7 5.8 all-to-all-start
  689.6 1.0 convolution_bitcast_fusion.2
  690.6 1.0 reshape.1222
  692.3 1.1 broadcast_in_dim.461
  694.3 5.4 all-to-all-done
  699.8 0.8 reshape.1224
  702.0 1.0 fusion.14
  703.1 0.9 fusion.15
  (368 shorter events, 37.4 us)
Async XLA Ops:
  0.6 6.1 copy-start
  0.6 6.3 copy-start.6
  0.7 6.7 copy-start.4
  1.4 63.8 %copy-start.81 = (s32[5]{0:T(128)}, s32[5]{0:T(128)S(1)}, u32[]{:S(2)}) copy-start(s32[5]{0:T(128)S(1)} %broadcast_add_fusion) | copy-start | bytes 64
  2.0 63.2 %copy-start.83 = (pred[5]{0:T(512)(128)(4,1)}, pred[5]{0:T(512)(128)(4,1)S(1)}, u32[]{:S(2)}) copy-start(pred[5]{0:T(512)(128)(4,1)S(1)} %broadcast_compare_fusion) | copy-start | bytes 19
  2.7 512.0 %copy-start.75 = (s32[5]{0:T(128)}, s32[5]{0:T(128)S(1)}, u32[]{:S(2)}) copy-start(s32[5]{0:T(128)S(1)} %broadcast_add_fusion.1) | copy-start | bytes 64
  3.4 511.4 %copy-start.77 = (pred[5]{0:T(512)(128)(4,1)}, pred[5]{0:T(512)(128)(4,1)S(1)}, u32[]{:S(2)}) copy-start(pred[5]{0:T(512)(128)(4,1)S(1)} %broadcast_compare_fusion.1) | copy-start | bytes 19
  5.6 2.1 copy-start.11
  7.7 532.2 %copy-start.20 = (bf16[1,128,320]{1,2,0:T(8,128)(2,1)}, bf16[1,128,320]{1,2,0:T(8,128)(2,1)S(1)}, u32[]{:S(2)}) copy-start(bf16[1,128,320]{1,2,0:T(8,128)(2,1)S(1)} %get-tuple-element.51) | copy-start | bytes 245764
  7.8 604.5 %copy-start.32 = (pred[128,128]{0,1:T(8,128)(4,1)}, pred[128,128]{0,1:T(8,128)(4,1)S(1)}, u32[]{:S(2)}) copy-start(pred[128,128]{0,1:T(8,128)(4,1)S(1)} %iota_compare_fusion.2) | copy-start | bytes 49156
  7.8 532.1 %copy-start.22 = (bf16[1,128,320]{1,2,0:T(8,128)(2,1)}, bf16[1,128,320]{1,2,0:T(8,128)(2,1)S(1)}, u32[]{:S(2)}) copy-start(bf16[1,128,320]{1,2,0:T(8,128)(2,1)S(1)} %slice.66) | copy-start | bytes 245764
  7.9 2.3 copy-start.88
  9.3 532.0 %copy-start.40 = (pred[256,5]{0,1:T(8,128)(4,1)}, pred[256,5]{0,1:T(8,128)(4,1)S(1)}, u32[]{:S(2)}) copy-start(pred[256,5]{0,1:T(8,128)(4,1)S(1)} %broadcast_in_dim.420) | copy-start | bytes 3844
  65.9 25.4 %copy-start.64 = (bf16[4,5,64]{2,1,0:T(8,128)(2,1)}, bf16[4,5,64]{2,1,0:T(8,128)(2,1)S(1)}, u32[]{:S(2)}) copy-start(bf16[4,5,64]{2,1,0:T(8,128)(2,1)S(1)} %get-tuple-element.78) | copy-start | bytes 7684
  90.4 451.5 %copy-start.99 = (pred[4,64]{1,0:T(4,128)(4,1)}, pred[4,64]{1,0:T(4,128)(4,1)S(1)}, u32[]{:S(2)}) copy-start(pred[4,64]{1,0:T(4,128)(4,1)S(1)} %iota_compare_fusion.5) | copy-start | bytes 772
  90.6 451.3 %copy-start.57 = (f32[5,4,64]{2,1,0:T(4,128)}, f32[5,4,64]{2,1,0:T(4,128)S(1)}, u32[]{:S(2)}) copy-start(f32[5,4,64]{2,1,0:T(4,128)S(1)} %get-tuple-element.82) | copy-start | bytes 15364
  90.8 451.1 %copy-start.54 = (f32[5,4]{1,0:T(8,128)}, f32[5,4]{1,0:T(8,128)S(1)}, u32[]{:S(2)}) copy-start(f32[5,4]{1,0:T(8,128)S(1)} %log_add_fusion.4) | copy-start | bytes 244
  515.5 23.4 %copy-start.28 = (bf16[32,5,64]{2,1,0:T(8,128)(2,1)}, bf16[32,5,64]{2,1,0:T(8,128)(2,1)S(1)}, u32[]{:S(2)}) copy-start(bf16[32,5,64]{2,1,0:T(8,128)(2,1)S(1)} %get-tuple-element.70) | copy-start | bytes 61444
  539.1 2.1 copy-start.26
  539.2 2.8 copy-start.37
  539.9 3.9 copy-start.38
  540.2 33.3 %copy-start.1 = (f32[5,128,128]{1,2,0:T(8,128)}, f32[5,128,128]{1,2,0:T(8,128)S(1)}, u32[]{:S(2)}) copy-start(f32[5,128,128]{1,2,0:T(8,128)S(1)} %get-tuple-element.86) | copy-start | bytes 983044
  540.3 3.5 copy-start.39
  540.5 3.3 copy-start.46
  541.2 2.6 copy-start.50
  571.5 3.7 copy-start.55
  575.2 6.5 copy-start.56
  575.2 6.5 copy-start.60
  575.2 6.5 copy-start.62
  575.2 6.5 copy-start.68
  575.2 6.5 copy-start.89
  582.8 3.9 copy-start.65
  583.8 14.9 %copy-start.74 = (s32[5]{0:T(128)S(1)}, s32[5]{0:T(128)}, u32[]{:S(2)}) copy-start(s32[5]{0:T(128)} %param.20) | copy-start | bytes 64
  583.8 14.9 %copy-start.76 = (s32[5]{0:T(128)S(1)}, s32[5]{0:T(128)}, u32[]{:S(2)}) copy-start(s32[5]{0:T(128)} %copy-done.75) | copy-start | bytes 64
  583.8 15.6 %copy-start.51 = (f32[256,5]{0,1:T(8,128)S(1)}, f32[256,5]{0,1:T(8,128)}, u32[]{:S(2)}) copy-start(f32[256,5]{0,1:T(8,128)} %copy-done.50) | copy-start | bytes 15364
  583.8 16.3 %copy-start.5 = (bf16[1,256,320]{1,2,0:T(8,128)(2,1)S(1)}, bf16[1,256,320]{1,2,0:T(8,128)(2,1)}, u32[]{:S(2)}) copy-start(bf16[1,256,320]{1,2,0:T(8,128)(2,1)} %param.18) | copy-start | bytes 491524
  593.0 88.6 %all-to-all-start.1 = ((bf16[16,2,1280]{2,1,0:T(2,128)(2,1)}), bf16[16,2,1280]{2,1,0:T(2,128)(2,1)}, u32[]{:S(2)}, u32[]{:S(2)}) async-start(bf16[16,2,1280]{2,1,0:T(2,128)(2,1)} %reshape.1221), calls=%async_computation.1 | async-start | bytes 163840 | tf_op jit(solution)/shard_map/all_to_all | solution.py:36
  603.4 2.8 copy-start.78
  608.8 3.4 copy-start.36
  608.8 3.4 copy-start.86
  608.8 3.5 copy-start.2
  608.8 3.5 copy-start.29
  608.8 3.5 copy-start.44
  608.8 3.5 copy-start.69
  608.8 3.5 copy-start.92
  608.8 3.5 copy-start.95
  610.1 2.5 copy-start.21
  610.1 3.4 copy-start.23
  612.4 3.2 copy-start.19
  625.7 3.8 copy-start.10
  627.7 8.1 %copy-start.8 = (f32[1,256,320]{2,1,0:T(8,128)S(1)}, f32[1,256,320]{2,1,0:T(8,128)}, u32[]{:S(2)}) copy-start(f32[1,256,320]{2,1,0:T(8,128)} %copy.290) | copy-start | bytes 983044
  627.7 8.1 %copy-start.9 = (f32[1,256,320]{2,1,0:T(8,128)S(1)}, f32[1,256,320]{2,1,0:T(8,128)}, u32[]{:S(2)}) copy-start(f32[1,256,320]{2,1,0:T(8,128)} %copy.294) | copy-start | bytes 983044
  627.7 8.1 %copy-start.17 = (f32[1,128,320]{2,1,0:T(8,128)S(1)}, f32[1,128,320]{2,1,0:T(8,128)}, u32[]{:S(2)}) copy-start(f32[1,128,320]{2,1,0:T(8,128)} %copy.299) | copy-start | bytes 491524
  635.8 2.3 copy-start.96
  635.8 2.3 copy-start.97
  635.8 2.3 copy-start.98
  638.1 49.9 %copy-start.16 = (bf16[1,256,320]{2,1,0:T(8,128)(2,1)S(1)}, bf16[1,256,320]{2,1,0:T(8,128)(2,1)}, u32[]{:S(2)}) copy-start(bf16[1,256,320]{2,1,0:T(8,128)(2,1)} %get-tuple-element.46) | copy-start | bytes 491524
  638.1 50.7 %copy-start.15 = (bf16[1,256,320]{2,1,0:T(8,128)(2,1)S(1)}, bf16[1,256,320]{2,1,0:T(8,128)(2,1)}, u32[]{:S(2)}) copy-start(bf16[1,256,320]{2,1,0:T(8,128)(2,1)} %get-tuple-element.45) | copy-start | bytes 491524
  638.1 51.5 %copy-start.3 = (f32[5,128,128]{1,2,0:T(8,128)S(1)}, f32[5,128,128]{1,2,0:T(8,128)}, u32[]{:S(2)}) copy-start(f32[5,128,128]{1,2,0:T(8,128)} %copy-done.1) | copy-start | bytes 983044
  638.1 51.5 %copy-start.33 = (pred[128,128]{0,1:T(8,128)(4,1)S(1)}, pred[128,128]{0,1:T(8,128)(4,1)}, u32[]{:S(2)}) copy-start(pred[128,128]{0,1:T(8,128)(4,1)} %copy-done.32) | copy-start | bytes 49156
  638.1 51.5 %copy-start.45 = (bf16[1,128,320]{1,2,0:T(8,128)(2,1)S(1)}, bf16[1,128,320]{1,2,0:T(8,128)(2,1)}, u32[]{:S(2)}) copy-start(bf16[1,128,320]{1,2,0:T(8,128)(2,1)} %get-tuple-element.49) | copy-start | bytes 245764
  638.1 51.5 %copy-start.71 = (f32[5]{0:T(128)S(1)}, f32[5]{0:T(128)}, u32[]{:S(2)}) copy-start(f32[5]{0:T(128)} %copy-done.67) | copy-start | bytes 64
  638.1 51.5 %copy-start.93 = (f32[5,128]{1,0:T(8,128)S(1)}, f32[5,128]{1,0:T(8,128)}, u32[]{:S(2)}) copy-start(f32[5,128]{1,0:T(8,128)} %get-tuple-element.88) | copy-start | bytes 7684
  681.7 18.1 %all-to-all-start = ((bf16[16,2,10240]{2,1,0:T(2,128)(2,1)}), bf16[16,2,10240]{2,1,0:T(2,128)(2,1)S(1)}, u32[]{:S(2)}, u32[]{:S(2)}) async-start(bf16[16,2,10240]{2,1,0:T(2,128)(2,1)} %reshape.1223), calls=%async_computation | async-start | bytes 1310720 | tf_op jit(solution)/shard_map/all_to_all | solution.py:36
  (40 other events, 55.8 us)
where the time goes:
time: 705 us; the launch traced here: 704 us
  local copies, waits for them, and re-layouts  537 us (76%)
  blocking collectives  113 us (16%)
  matrix products  18.4 us (3%)
  other arithmetic  17 us (2%)
  starting transfers between devices  11.3 us (2%)
    gather x29, local copies, waits for them, and re-layouts, select_rows(): return jnp.take_along_axis(shaped, picker, axis=1)[:, 0]  485 us
    psum x5, blocking collectives, one_axis_at_a_time(): array = lax.psum(array, axis)  43.3 us
    all_gather x1, blocking collectives, sent_together(): filled = lax.all_gather(both, axis, axis=dim, tiled=True)  23.7 us
    all_gather x1, blocking collectives, per_device(): lax.all_gather(mid_values, GROUP, axis=0, tiled=True)  23.1 us
    all_gather x1, blocking collectives, per_device(): lax.all_gather(mid_keys, GROUP, axis=0, tiled=True)  22.6 us
    broadcast_in_dim x38, local copies, waits for them, and re-layouts, place_rows(): jnp.where(marked, source[:, None], jnp.asarray(filler, source.dtype))  20.4 us
  transfers between devices with their start and end apart: 2, of which 1 were waited for; matrix products, arithmetic and copies ran while one was open for 6% of the time, Pallas kernels for 0%

commit v1 on v0

--- a/solution.py
+++ b/solution.py
@@ -4,6 +4,7 @@
 from jax import lax
 from jax.sharding import Mesh
 from jax.sharding import PartitionSpec as P
+from jax.lax import all_to_all, psum
 
 HEADS = 40
 R_MID = 8
@@ -187,7 +188,7 @@
     mid_keys = select_rows(key_rows, R_MID, off_mid)
     mid_values = select_rows(value_rows, R_MID, off_mid)
     mid_all_keys, mid_all_values = (
-        lax.all_gather(mid_keys, GROUP, axis=0, tiled=True),
+        jnp.concatenate(all_to_all(jnp.stack(psum(1, GROUP) * [mid_keys]), GROUP, 0, 0), axis=0),
         lax.all_gather(mid_values, GROUP, axis=0, tiled=True),
     )
     mid_lse, mid_out = blocked_forward(

time: 705 us -> 666 us (0.945)
  blocking collectives: 113 us -> 89.6 us
  local copies, waits for them, and re-layouts: 537 us -> 523 us
  starting transfers between devices: 11.3 us -> 19.2 us
    all_gather x1 -> x0, blocking collectives: 22.6 us -> none  [per_device(): lax.all_gather(mid_keys, GROUP, axis=0, tiled=True)]
    all_to_all x0 -> x1, starting transfers between devices: none -> 7.39 us  [per_device(): all_to_all(jnp.stack(psum(1, GROUP) * [mid_keys]), GROUP, 0, 0)]
  transfers between devices with their start and end apart: 2 -> 3, of which waited for: 1 -> 1; matrix products, arithmetic and copies ran while one was open for 6% -> 13% of each run, Pallas kernels for 0% -> 0%
where the time goes in v1:
time: 666 us; the launch traced here: 665 us
  local copies, waits for them, and re-layouts  523 us (79%)
  blocking collectives  89.6 us (13%)
  starting transfers between devices  19.2 us (3%)
  matrix products  13.1 us (2%)
  other arithmetic  12.5 us (2%)
    gather x29, local copies, waits for them, and re-layouts, select_rows(): return jnp.take_along_axis(shaped, picker, axis=1)[:, 0]  485 us
    psum x5, blocking collectives, one_axis_at_a_time(): array = lax.psum(array, axis)  43.5 us
    all_gather x1, blocking collectives, sent_together(): filled = lax.all_gather(both, axis, axis=dim, tiled=True)  23.6 us
    all_gather x1, blocking collectives, per_device(): lax.all_gather(mid_values, GROUP, axis=0, tiled=True)  22.6 us
    broadcast_in_dim x38, local copies, waits for them, and re-layouts, place_rows(): jnp.where(marked, source[:, None], jnp.asarray(filler, source.dtype))  13.5 us
  transfers between devices with their start and end apart: 3, of which 1 were waited for; matrix products, arithmetic and copies ran while one was open for 13% of the time, Pallas kernels for 0%

profile of v1, /device:TPU:8, one launch (start us, length us, event | category | flops | bytes accessed | tf_op | source)
XLA Modules:
  0.0 665.1 jit_solution(3353676060443782736)
XLA Ops:
  0.6 0.7 broadcast_add_fusion.1
  2.0 0.7 select_bitcast_fusion
  3.5 105.5 %gather_fusion = bf16[10240]{0:T(1024)(128)(2,1)S(1)} fusion(bf16[32,8,5,64]{3,2,1,0:T(8,128)(2,1)S(1)} %reshape_reshape_squeeze.24, s32[10240]{0:T(1024)S(1)} %reshape.1156), kind=kCustom, calls=%fused_computation.clone | custom fusion | bytes 204800 | tf_op jit(solution)/shard_map/jit(take_along_axis)/gather | solution.py:55
  109.5 105.5 %gather_fusion.1 = bf16[10240]{0:T(1024)(128)(2,1)S(1)} fusion(bf16[32,8,5,64]{3,2,1,0:T(8,128)(2,1)S(1)} %reshape_reshape_squeeze.25, s32[10240]{0:T(1024)S(1)} %reshape.1156), kind=kCustom, calls=%fused_computation.4.clone | custom fusion | bytes 204800 | tf_op jit(solution)/shard_map/jit(take_along_axis)/gather | solution.py:55
  215.5 105.5 %gather_fusion.5 = bf16[10240]{0:T(1024)(128)(2,1)S(1)} fusion(bf16[32,8,5,64]{3,2,1,0:T(8,128)(2,1)S(1)} %reshape_reshape_squeeze.29, s32[10240]{0:T(1024)S(1)} %reshape.1156), kind=kCustom, calls=%fused_computation.5.clone | custom fusion | bytes 204800 | tf_op jit(solution)/shard_map/jit(take_along_axis)/gather | solution.py:55
  321.5 105.5 %gather_fusion.7 = bf16[10240]{0:T(1024)(128)(2,1)S(1)} fusion(bf16[32,8,5,64]{3,2,1,0:T(8,128)(2,1)S(1)} %reshape_reshape_squeeze.30, s32[10240]{0:T(1024)S(1)} %reshape.1156), kind=kCustom, calls=%fused_computation.6.clone | custom fusion | bytes 204800 | tf_op jit(solution)/shard_map/jit(take_along_axis)/gather | solution.py:55
  427.2 0.8 select_bitcast_fusion.1
  428.1 1.1 reshape.1226
  429.2 7.4 %all-to-all-start = ((bf16[16,2,5120]{2,1,0:T(2,128)(2,1)}), bf16[16,2,5120]{2,1,0:T(2,128)(2,1)S(1)}, u32[]{:S(2)}, u32[]{:S(2)}) async-start(bf16[16,2,5120]{2,1,0:T(2,128)(2,1)} %reshape.1226), calls=%async_computation | async-start | bytes 655360 | tf_op jit(solution)/shard_map/all_to_all | solution.py:191
  438.6 13.7 %gather_fusion.2 = bf16[1280]{0:T(1024)(128)(2,1)S(1)} fusion(bf16[4,64,5,64]{1,0,3,2:T(4,128)(2,1)S(1)} %reshape_reshape_squeeze.26, s32[1280]{0:T(1024)S(1)} %reshape.1168), kind=kCustom, calls=%fused_computation.1.clone | custom fusion | bytes 25600 | tf_op jit(solution)/shard_map/jit(take_along_axis)/gather | solution.py:55
  452.4 13.7 %gather_fusion.3 = bf16[1280]{0:T(1024)(128)(2,1)S(1)} fusion(bf16[4,64,5,64]{1,0,3,2:T(4,128)(2,1)S(1)} %reshape_reshape_squeeze.27, s32[1280]{0:T(1024)S(1)} %reshape.1168), kind=kCustom, calls=%fused_computation.7.clone | custom fusion | bytes 25600 | tf_op jit(solution)/shard_map/jit(take_along_axis)/gather | solution.py:55
  466.2 13.7 %gather_fusion.4 = bf16[1280]{0:T(1024)(128)(2,1)S(1)} fusion(bf16[4,64,5,64]{1,0,3,2:T(4,128)(2,1)S(1)} %reshape_reshape_squeeze.28, s32[1280]{0:T(1024)S(1)} %reshape.1168), kind=kCustom, calls=%fused_computation.8.clone | custom fusion | bytes 25600 | tf_op jit(solution)/shard_map/jit(take_along_axis)/gather | solution.py:55
  479.9 13.7 %gather_fusion.10 = bf16[1280]{0:T(1024)(128)(2,1)S(1)} fusion(bf16[4,64,5,64]{1,0,3,2:T(4,128)(2,1)S(1)} %reshape_reshape_squeeze.31, s32[1280]{0:T(1024)S(1)} %reshape.1168), kind=kCustom, calls=%fused_computation.9.clone | custom fusion | bytes 25600 | tf_op jit(solution)/shard_map/jit(take_along_axis)/gather | solution.py:55
  494.4 23.6 %all_gather.6 = bf16[64,10,64]{2,1,0:T(8,128)(2,1)S(1)} all-gather(bf16[4,10,64]{2,1,0:T(8,128)(2,1)S(1)} %pad_maximum_fusion.3), channel_id=1, replica_groups=mesh['dp'=2,'group_0'=4,'group_1'=4,'seq_0'=4,'seq_1'=2] {'group_0','gro..., dimensions={0}, use_global_device_ids=true | all-gather | bytes 87040 | tf_op jit(solution)/shard_map/all_gather | solution.py:20
  519.3 1.1 broadcast_in_dim.438
  523.9 0.7 broadcast_in_dim.463
  525.8 0.9 copy.305
  527.1 0.8 copy.294
  528.1 0.8 copy.293
  528.9 0.8 copy.304
  529.8 0.8 copy.300
  530.6 22.6 %all-gather = bf16[512,1,5,64]{3,0,2,1:T(8,128)(2,1)S(1)} all-gather(bf16[32,1,5,64]{3,0,2,1:T(8,128)(2,1)S(1)} %copy.297), channel_id=2, replica_groups=mesh['dp'=2,'group_0'=4,'group_1'=4,'seq_0'=4,'seq_1'=2] {'group_0','gro..., dimensions={0}, use_global_device_ids=true | all-gather | bytes 348160 | tf_op jit(solution)/shard_map/all_gather | solution.py:192
  554.4 1.2 select_reduce_fusion.1
  556.2 0.7 subtract_exponential_fusion.1
  556.9 1.4 subtract_exponential_fusion
  559.2 1.0 copy.307
  560.3 1.5 fusion.33
  562.0 0.8 multiply_reduce_fusion.2
  563.9 2.2 gather_fusion.6
  566.3 2.7 gather_fusion.8
  570.3 0.9 convolution_bitcast_fusion.5
  571.5 0.9 gather_fusion.9
  572.6 0.9 gather_fusion.11
  573.8 0.9 fusion.18
  574.8 0.9 fusion.17
  575.7 0.7 convolution_bitcast_fusion.6
  576.8 0.9 convolution_bitcast_fusion.3
  577.7 0.8 fusion.119
  578.5 0.7 copy.366
  579.3 0.7 copy.335
  580.4 1.7 reshape.1230
  582.4 0.8 reshape.1228
  583.2 6.0 all-to-all-start.2
  591.2 0.8 copy.310
  593.1 0.8 copy.311
  594.2 0.9 copy.306
  595.2 0.9 copy.301
  596.2 1.0 broadcast_in_dim.429
  597.2 1.8 fusion.29
  599.2 10.1 %psum.35 = f32[3,40]{1,0:T(4,128)S(1)} all-reduce(f32[3,40]{1,0:T(4,128)S(1)} %dynamic_update_slice.3), channel_id=1, replica_groups=mesh['dp'=2,'group_0'=4,'group_1'=4,'seq_0'=4,'seq_1'=2] {'dp'}, use_global_device_ids=true, to_apply=%region_17.22 | all-reduce | flops 120 | bytes 960 | tf_op jit(solution)/shard_map/psum | solution.py:26
  609.3 10.4 %psum.36 = f32[3,40]{1,0:T(4,128)S(1)} all-reduce(f32[3,40]{1,0:T(4,128)S(1)} %psum.35), channel_id=1, replica_groups=mesh['dp'=2,'group_0'=4,'group_1'=4,'seq_0'=4,'seq_1'=2] {'group_0'}, use_global_device_ids=true, to_apply=%region_18.23 | all-reduce | flops 120 | bytes 960 | tf_op jit(solution)/shard_map/psum | solution.py:26
  619.7 8.8 %psum.37 = f32[3,40]{1,0:T(4,128)S(1)} all-reduce(f32[3,40]{1,0:T(4,128)S(1)} %psum.36), channel_id=1, replica_groups=mesh['dp'=2,'group_0'=4,'group_1'=4,'seq_0'=4,'seq_1'=2] {'group_1'}, use_global_device_ids=true, to_apply=%region_19.24 | all-reduce | flops 120 | bytes 960 | tf_op jit(solution)/shard_map/psum | solution.py:26
  628.5 11.8 %psum.38 = f32[3,40]{1,0:T(4,128)S(1)} all-reduce(f32[3,40]{1,0:T(4,128)S(1)} %psum.37), channel_id=1, replica_groups=mesh['dp'=2,'group_0'=4,'group_1'=4,'seq_0'=4,'seq_1'=2] {'seq_0'}, use_global_device_ids=true, to_apply=%region_20.25 | all-reduce | flops 120 | bytes 960 | tf_op jit(solution)/shard_map/psum | solution.py:26
  640.3 2.5 psum.39
  642.7 5.8 all-to-all-start.1
  649.1 0.8 copy.349
  649.9 0.8 copy.350
  650.7 1.0 convolution_bitcast_fusion.2
  651.7 1.0 reshape.1229
  653.4 1.1 broadcast_in_dim.461
  655.4 5.4 all-to-all-done.1
  660.9 0.8 reshape.1231
  663.1 1.0 fusion.14
  664.2 0.9 fusion.15
  (389 shorter events, 26.0 us)
Async XLA Ops:
  0.6 2.4 copy-start.9
  1.3 437.1 %copy-start.84 = (s32[5]{0:T(128)}, s32[5]{0:T(128)S(1)}, u32[]{:S(2)}) copy-start(s32[5]{0:T(128)S(1)} %broadcast_add_fusion.1) | copy-start | bytes 64
  2.0 436.4 %copy-start.86 = (pred[5]{0:T(512)(128)(4,1)}, pred[5]{0:T(512)(128)(4,1)S(1)}, u32[]{:S(2)}) copy-start(pred[5]{0:T(512)(128)(4,1)S(1)} %broadcast_compare_fusion.1) | copy-start | bytes 19
  3.4 105.6 %copy-start = (bf16[1,256,320]{1,2,0:T(8,128)(2,1)S(1)}, bf16[1,256,320]{1,2,0:T(8,128)(2,1)}, u32[]{:S(2)}) copy-start(bf16[1,256,320]{1,2,0:T(8,128)(2,1)} %param.16) | copy-start | bytes 491524
  109.5 105.6 %copy-start.4 = (bf16[1,256,320]{1,2,0:T(8,128)(2,1)S(1)}, bf16[1,256,320]{1,2,0:T(8,128)(2,1)}, u32[]{:S(2)}) copy-start(bf16[1,256,320]{1,2,0:T(8,128)(2,1)} %param.17) | copy-start | bytes 491524
  215.5 105.6 %copy-start.3 = (bf16[1,256,320]{1,2,0:T(8,128)(2,1)S(1)}, bf16[1,256,320]{1,2,0:T(8,128)(2,1)}, u32[]{:S(2)}) copy-start(bf16[1,256,320]{1,2,0:T(8,128)(2,1)} %param.18) | copy-start | bytes 491524
  321.5 105.6 %copy-start.82 = (s32[5]{0:T(128)S(1)}, s32[5]{0:T(128)}, u32[]{:S(2)}) copy-start(s32[5]{0:T(128)} %param.20) | copy-start | bytes 64
  427.9 8.6 %copy-start.88 = (s32[5]{0:T(128)S(1)}, s32[5]{0:T(128)}, u32[]{:S(2)}) copy-start(s32[5]{0:T(128)} %param.21) | copy-start | bytes 64
  429.2 124.7 %all-to-all-start = ((bf16[16,2,5120]{2,1,0:T(2,128)(2,1)}), bf16[16,2,5120]{2,1,0:T(2,128)(2,1)S(1)}, u32[]{:S(2)}, u32[]{:S(2)}) async-start(bf16[16,2,5120]{2,1,0:T(2,128)(2,1)} %reshape.1226), calls=%async_computation | async-start | bytes 655360 | tf_op jit(solution)/shard_map/all_to_all | solution.py:191
  436.6 57.1 %copy-start.90 = (s32[5]{0:T(128)}, s32[5]{0:T(128)S(1)}, u32[]{:S(2)}) copy-start(s32[5]{0:T(128)S(1)} %broadcast_add_fusion) | copy-start | bytes 64
  436.6 57.1 %copy-start.92 = (pred[5]{0:T(512)(128)(4,1)}, pred[5]{0:T(512)(128)(4,1)S(1)}, u32[]{:S(2)}) copy-start(pred[5]{0:T(512)(128)(4,1)S(1)} %broadcast_compare_fusion) | copy-start | bytes 19
  437.5 85.0 %copy-start.14 = (bf16[1,128,320]{1,2,0:T(8,128)(2,1)}, bf16[1,128,320]{1,2,0:T(8,128)(2,1)S(1)}, u32[]{:S(2)}) copy-start(bf16[1,128,320]{1,2,0:T(8,128)(2,1)S(1)} %get-tuple-element.51) | copy-start | bytes 245764
  437.5 90.4 %copy-start.33 = (pred[128,128]{0,1:T(8,128)(4,1)}, pred[128,128]{0,1:T(8,128)(4,1)S(1)}, u32[]{:S(2)}) copy-start(pred[128,128]{0,1:T(8,128)(4,1)S(1)} %iota_compare_fusion.2) | copy-start | bytes 49156
  437.5 85.0 %copy-start.16 = (bf16[1,128,320]{1,2,0:T(8,128)(2,1)}, bf16[1,128,320]{1,2,0:T(8,128)(2,1)S(1)}, u32[]{:S(2)}) copy-start(bf16[1,128,320]{1,2,0:T(8,128)(2,1)S(1)} %slice.66) | copy-start | bytes 245764
  437.7 85.9 %copy-start.94 = (pred[8,5]{0,1:T(8,128)(4,1)}, pred[8,5]{0,1:T(8,128)(4,1)S(1)}, u32[]{:S(2)}) copy-start(pred[8,5]{0,1:T(8,128)(4,1)S(1)} %iota_compare_fusion.4) | copy-start | bytes 124
  437.7 90.2 %copy-start.27 = (bf16[1,128,320]{1,2,0:T(8,128)(2,1)}, bf16[1,128,320]{1,2,0:T(8,128)(2,1)S(1)}, u32[]{:S(2)}) copy-start(bf16[1,128,320]{1,2,0:T(8,128)(2,1)S(1)} %slice.73) | copy-start | bytes 245764
  438.3 90.6 %copy-start.43 = (pred[256,5]{0,1:T(8,128)(4,1)}, pred[256,5]{0,1:T(8,128)(4,1)S(1)}, u32[]{:S(2)}) copy-start(pred[256,5]{0,1:T(8,128)(4,1)S(1)} %broadcast_in_dim.420) | copy-start | bytes 3844
  494.4 26.1 %copy-start.73 = (bf16[4,5,64]{2,1,0:T(8,128)(2,1)}, bf16[4,5,64]{2,1,0:T(8,128)(2,1)S(1)}, u32[]{:S(2)}) copy-start(bf16[4,5,64]{2,1,0:T(8,128)(2,1)S(1)} %get-tuple-element.78) | copy-start | bytes 7684
  518.1 2.7 copy-start.103
  518.3 2.5 copy-start.64
  518.5 5.2 copy-start.62
  520.9 2.0 copy-start.108
  521.8 5.0 copy-start.20
  522.5 33.6 %copy-start.39 = (f32[5,128]{1,0:T(8,128)}, f32[5,128]{1,0:T(8,128)S(1)}, u32[]{:S(2)}) copy-start(f32[5,128]{1,0:T(8,128)S(1)} %log_add_fusion.6) | copy-start | bytes 7684
  522.8 53.7 %copy-start.1 = (f32[5,128,128]{1,2,0:T(8,128)}, f32[5,128,128]{1,2,0:T(8,128)S(1)}, u32[]{:S(2)}) copy-start(f32[5,128,128]{1,2,0:T(8,128)S(1)} %get-tuple-element.86) | copy-start | bytes 983044
  522.9 33.2 %copy-start.41 = (f32[5,128]{1,0:T(8,128)}, f32[5,128]{1,0:T(8,128)S(1)}, u32[]{:S(2)}) copy-start(f32[5,128]{1,0:T(8,128)S(1)} %log_add_fusion.7) | copy-start | bytes 7684
  523.7 6.1 copy-start.50
  527.1 3.5 copy-start.7
  528.1 26.2 %copy-start.8 = (f32[5,128,64]{1,2,0:T(8,128)}, f32[5,128,64]{1,2,0:T(8,128)S(1)}, u32[]{:S(2)}) copy-start(f32[5,128,64]{1,2,0:T(8,128)S(1)} %fusion.47) | copy-start | bytes 491524
  555.9 2.4 copy-start.60
  556.1 2.2 copy-start.58
  560.3 2.8 copy-start.57
  560.3 3.5 copy-start.61
  560.3 3.5 copy-start.67
  560.3 3.5 copy-start.76
  560.3 3.5 copy-start.95
  563.7 12.8 %copy-start.100 = (f32[5,128]{1,0:T(8,128)}, f32[5,128]{1,0:T(8,128)S(1)}, u32[]{:S(2)}) copy-start(f32[5,128]{1,0:T(8,128)S(1)} %get-tuple-element.88) | copy-start | bytes 7684
  566.2 2.9 copy-start.83
  566.2 2.9 copy-start.85
  566.2 2.9 copy-start.87
  566.3 3.0 copy-start.26
  572.4 2.2 copy-start.38
  572.5 2.4 copy-start.74
  572.5 3.3 copy-start.36
  572.6 3.9 copy-start.28
  572.6 3.9 copy-start.34
  572.6 3.9 copy-start.48
  572.6 4.2 copy-start.15
  573.5 4.2 copy-start.17
  573.5 5.0 copy-start.13
  580.4 8.9 %copy-start.29 = (f32[32,5,64]{2,0,1:T(8,128)S(1)}, f32[32,5,64]{2,0,1:T(8,128)}, u32[]{:S(2)}) copy-start(f32[32,5,64]{2,0,1:T(8,128)} %convolution_bitcast_fusion.5) | copy-start | bytes 122884
  583.2 59.5 %all-to-all-start.2 = ((bf16[16,2,1280]{2,1,0:T(2,128)(2,1)}), bf16[16,2,1280]{2,1,0:T(2,128)(2,1)}, u32[]{:S(2)}, u32[]{:S(2)}) async-start(bf16[16,2,1280]{2,1,0:T(2,128)(2,1)} %reshape.1228), calls=%async_computation.2 | async-start | bytes 163840 | tf_op jit(solution)/shard_map/all_to_all | solution.py:37
  590.2 1.9 copy-start.5
  590.2 1.9 copy-start.21
  592.0 1.9 copy-start.54
  593.1 2.0 copy-start.53
  594.0 2.1 copy-start.23
  597.2 1.8 copy-start.106
  597.2 1.9 copy-start.107
  599.0 51.7 %copy-start.2 = (f32[5,128,128]{1,2,0:T(8,128)S(1)}, f32[5,128,128]{1,2,0:T(8,128)}, u32[]{:S(2)}) copy-start(f32[5,128,128]{1,2,0:T(8,128)} %copy-done.1) | copy-start | bytes 983044
  599.0 51.7 %copy-start.49 = (bf16[1,128,320]{1,2,0:T(8,128)(2,1)S(1)}, bf16[1,128,320]{1,2,0:T(8,128)(2,1)}, u32[]{:S(2)}) copy-start(bf16[1,128,320]{1,2,0:T(8,128)(2,1)} %get-tuple-element.49) | copy-start | bytes 245764
  599.0 51.7 %copy-start.80 = (f32[5]{0:T(128)S(1)}, f32[5]{0:T(128)}, u32[]{:S(2)}) copy-start(f32[5]{0:T(128)} %get-tuple-element.64) | copy-start | bytes 64
  599.0 51.7 %copy-start.101 = (f32[5,128]{1,0:T(8,128)S(1)}, f32[5,128]{1,0:T(8,128)}, u32[]{:S(2)}) copy-start(f32[5,128]{1,0:T(8,128)} %copy-done.100) | copy-start | bytes 7684
  642.7 18.1 %all-to-all-start.1 = ((bf16[16,2,10240]{2,1,0:T(2,128)(2,1)}), bf16[16,2,10240]{2,1,0:T(2,128)(2,1)S(1)}, u32[]{:S(2)}, u32[]{:S(2)}) async-start(bf16[16,2,10240]{2,1,0:T(2,128)(2,1)} %reshape.1230), calls=%async_computation.1 | async-start | bytes 1310720 | tf_op jit(solution)/shard_map/all_to_all | solution.py:37
  (49 other events, 69.7 us)
